TPU v7x, 512 devices: a whole 4x4x16 slice. The times are simulated.
512 devices in a mesh: dp: 64 (over z, x), head: 8 (over y, core).
Axes of the slice: x: 4, y: 4, z: 16, core: 2. Of those that a mesh axis runs over, the one named last changes fastest.
Arguments:
- queries: bfloat16 [16384, 8192], P('dp', 'head'), may hold values from -6 to 6
- keys: bfloat16 [16384, 1024], P('dp', 'head'), may hold values from -6 to 6
- values: bfloat16 [16384, 1024], P('dp', 'head'), may hold values from -6 to 6
- output_grad: bfloat16 [16384, 4096], P('dp', 'head'), may hold values from -6 to 6
- out_weight: bfloat16 [8192, 4096], P(('head', 'dp')), may hold values from -0.0625 to 0.0625
- lengths: int32 [64], replicated, may hold values from 1 to 512, 16384 in all
Outputs:
- layer_out: bfloat16 [16384, 4096], P('dp', 'head')
- query_grad: bfloat16 [16384, 8192], P('dp', 'head')
- key_grad: bfloat16 [16384, 1024], P('dp', 'head')
- value_grad: bfloat16 [16384, 1024], P('dp', 'head')
Inputs may be any that keep to these rules, and one draw needn't show every extreme that they name: Each of the 64 lengths is at least 1 and at most 512, they sum to 16384, and one equals 512.
All inputs are finite; a program needn't handle non-finite values.
Results may differ from a plain program's by a relative error of at most 0.028.
Values may be sent and summed in bfloat16 or wider, within the bound.
No kernel may reach another device: no remote copies, remote signals or barrier semaphores. Data moves between devices by JAX's collectives and lax.ppermute only.
A program may use at most 128 MiB of HBM per device.

v0:
```python
import math

import jax
import jax.numpy as jnp
from jax import lax
from jax.sharding import Mesh
from jax.sharding import PartitionSpec as P

HD = 128
SPAN = 2
DP = ("dp_0", "dp_1")
HEAD_DP = ("head", "dp_0", "dp_1")


masked_score = -1e30


def gather_axes(x, axes, dim):
    filled = x
    for number in range(len(axes) - 1, -1, -1):
        filled = lax.all_gather(filled, axes[number], axis=dim, tiled=True)
    return filled


def in_order(pieces, dim):
    pieces = jnp.moveaxis(pieces, 0, dim)
    shape = pieces.shape
    return pieces.reshape(*shape[:dim], shape[dim] * shape[dim + 1], *shape[dim + 2 :])


def from_everyone(x, axis):
    size = lax.axis_size(axis)
    return lax.all_to_all(jnp.broadcast_to(x[None], (size, *x.shape)), axis, 0, 0, tiled=True)


def gather_directly(x, axis, dim):
    return in_order(from_everyone(x, axis), dim)


def passed_along(block, axis, distance):
    devices = range(lax.axis_size(axis))
    route = [(i - distance, i) for i in devices if i - distance in devices]
    return lax.ppermute(block, axis, route)


def in_blocks(x, dim, size):
    before, after = (x.shape[:dim], x.shape[dim + 1 :])
    return jnp.moveaxis(x.reshape(*before, size, -1, *after), dim, 0)


def sent_and_summed(x, axis, dim):
    pieces = in_blocks(x, dim, lax.axis_size(axis))
    arrived = lax.all_to_all(pieces, axis, split_axis=0, concat_axis=0, tiled=True)
    return arrived.astype(jnp.float32).sum(axis=0)


def doc_start(lengths, positions):
    doc_ends = jnp.cumsum(lengths)
    closed = doc_ends[None, :] <= positions[:, None]
    return jnp.sum(jnp.where(closed, lengths[None, :], 0), axis=1)


def attend(queries, key_rows, value_rows, d_attended, visible, head_dim):
    row_count = queries.shape[0]
    kv_heads = key_rows.shape[1] // head_dim
    group_ratio = queries.shape[1] // key_rows.shape[1]
    scaling = 1.0 / math.sqrt(head_dim)
    grouped = queries.reshape(row_count, kv_heads, group_ratio, head_dim)
    keyed = key_rows.reshape(-1, kv_heads, head_dim)
    valued = value_rows.reshape(-1, kv_heads, head_dim)
    upstream = d_attended.reshape(row_count, kv_heads, group_ratio, head_dim)
    scores = (
        jnp.einsum("tgrd,ngd->grtn", grouped, keyed, preferred_element_type=jnp.float32) * scaling
    )
    scores = jnp.where(visible[None, None], scores, masked_score)
    maximum = jnp.max(scores, axis=-1, keepdims=True)
    weights = jnp.exp(scores - maximum)
    shares = weights / jnp.sum(weights, axis=-1, keepdims=True)
    shares_low = shares.astype(jnp.bfloat16)
    attended = jnp.einsum(
        "grtn,ngd->tgrd", shares_low, valued, preferred_element_type=jnp.float32
    ).astype(jnp.bfloat16)
    row_dots = jnp.sum(upstream.astype(jnp.float32) * attended.astype(jnp.float32), axis=-1)
    d_shares = jnp.einsum("tgrd,ngd->grtn", upstream, valued, preferred_element_type=jnp.float32)
    dscore = (shares * (d_shares - jnp.transpose(row_dots, (1, 2, 0))[..., None]) * scaling).astype(
        jnp.bfloat16
    )
    query_grad = jnp.einsum(
        "grtn,ngd->tgrd", dscore, keyed, preferred_element_type=jnp.float32
    ).astype(jnp.bfloat16)
    key_part = jnp.einsum("grtn,tgrd->ngd", dscore, grouped, preferred_element_type=jnp.float32)
    value_part = jnp.einsum(
        "grtn,tgrd->ngd", shares_low, upstream, preferred_element_type=jnp.float32
    )
    return (
        attended.reshape(row_count, -1),
        query_grad.reshape(row_count, -1),
        key_part.reshape(-1, kv_heads * head_dim),
        value_part.reshape(-1, kv_heads * head_dim),
    )


def on_device(queries, keys, values, output_grad, out_weight, lengths):
    block_rows = queries.shape[0]
    device = lax.axis_index(DP)
    group_weight = gather_axes(out_weight, DP, 0)
    upstream_all = gather_directly(output_grad, "head", 1)
    d_attended = jnp.einsum(
        "tc,rc->tr", upstream_all, group_weight, preferred_element_type=jnp.float32
    ).astype(jnp.bfloat16)
    earlier = [passed_along((keys, values), DP, offset) for offset in range(1, SPAN + 1)]
    key_rows = jnp.concatenate([couple[0] for couple in earlier[::-1]] + [keys], axis=0)
    value_rows = jnp.concatenate([couple[1] for couple in earlier[::-1]] + [values], axis=0)
    owner_positions = device * block_rows + jnp.arange(block_rows, dtype=jnp.int32)
    owner_starts = doc_start(lengths, owner_positions)
    key_positions = (device - SPAN) * block_rows + jnp.arange(
        (SPAN + 1) * block_rows, dtype=jnp.int32
    )
    visible = (key_positions[None, :] >= owner_starts[:, None]) & (
        key_positions[None, :] <= owner_positions[:, None]
    )
    first_row = 0 * block_rows
    attended, query_grad, key_part, value_part = attend(
        queries, key_rows, value_rows, d_attended, visible, HD
    )
    padding = jnp.zeros((first_row, key_part.shape[1]), jnp.float32)
    attended, query_grad, key_all, value_all = (
        attended,
        query_grad,
        jnp.concatenate([padding, key_part], axis=0),
        jnp.concatenate([padding, value_part], axis=0),
    )
    projected = jnp.dot(attended, group_weight, preferred_element_type=jnp.float32)
    layer_out = sent_and_summed(projected.astype(jnp.bfloat16), "head", 1).astype(jnp.bfloat16)

    def block_of(all_rows, offset):
        return all_rows[(SPAN - offset) * block_rows : (SPAN - offset + 1) * block_rows]

    key_home = block_of(key_all, 0)
    value_home = block_of(value_all, 0)
    for offset in range(1, SPAN + 1):
        returned = (
            passed_along(block_of(key_all, offset).astype(jnp.bfloat16), DP, -offset).astype(
                jnp.float32
            ),
            passed_along(block_of(value_all, offset).astype(jnp.bfloat16), DP, -offset).astype(
                jnp.float32
            ),
        )
        key_home = key_home + returned[0]
        value_home = value_home + returned[1]
    return (layer_out, query_grad, key_home.astype(jnp.bfloat16), value_home.astype(jnp.bfloat16))


def solution(mesh):
    finer = Mesh(mesh.devices.reshape(16, 4, mesh.shape["head"]), ("dp_0", "dp_1", "head"))
    placed = (P(DP, "head"), P(DP, "head"), P(DP, "head"), P(DP, "head"), P(HEAD_DP, None), P())
    return jax.shard_map(
        on_device,
        mesh=finer,
        in_specs=placed,
        out_specs=(P(DP, "head"), P(DP, "head"), P(DP, "head"), P(DP, "head")),
        check_vma=False,
    )
```

profile of v0, /device:TPU:54, one launch (start us, length us, event | category | flops | bytes accessed | tf_op | source)
XLA Modules:
  0.0 191.5 jit_solution(2277917822769658784)
XLA Ops:
  7.2 13.9 %all_gather.6 = bf16[64,4096]{1,0:T(8,128)(2,1)} all-gather(bf16[16,4096]{1,0:T(8,128)(2,1)} %param.10), channel_id=1, replica_groups=mesh['dp_0'=16,'dp_1'=4,'head'=8] {'dp_1'}, dimensions={0}, use_global_device_ids=true | all-gather | bytes 655360 | tf_op jit(solution)/shard_map/all_gather | solution.py:21
  21.1 4.8 %collective-permute-start.3 = (bf16[256,128]{1,0:T(8,128)(2,1)}, bf16[256,128]{1,0:T(8,128)(2,1)S(1)}, u32[]{:S(2)}, u32[]{:S(2)}) collective-permute-start(bf16[256,128]{1,0:T(8,128)(2,1)} %param.7), channel_id=1, source_target_pairs={{0,8},{8,16},{16,24},{24,32},{32,40},{40,48},{48,56},{56,64},{64,7... | collective-permute-start | bytes 196616 | tf_op jit(solution)/shard_map/ppermute | solution.py:43
  26.0 2.8 %collective-permute-start.2 = (bf16[256,128]{1,0:T(8,128)(2,1)}, bf16[256,128]{1,0:T(8,128)(2,1)S(1)}, u32[]{:S(2)}, u32[]{:S(2)}) collective-permute-start(bf16[256,128]{1,0:T(8,128)(2,1)} %param.7), channel_id=1, source_target_pairs={{0,16},{8,24},{16,32},{24,40},{32,48},{40,56},{48,64},{56,72},{64,... | collective-permute-start | bytes 196616 | tf_op jit(solution)/shard_map/ppermute | solution.py:43
  29.7 4.2 %collective-permute-start.1 = (bf16[256,128]{0,1:T(8,128)(2,1)S(1)}, bf16[256,128]{0,1:T(8,128)(2,1)}, u32[]{:S(2)}, u32[]{:S(2)}) collective-permute-start(bf16[256,128]{0,1:T(8,128)(2,1)S(1)} %copy.60), channel_id=1, source_target_pairs={{0,8},{8,16},{16,24},{24,32},{32,40},{40,48},{48,56},{56,64},{64,7... | collective-permute-start | bytes 196616 | tf_op jit(solution)/shard_map/ppermute | solution.py:43
  33.9 3.7 %collective-permute-start = (bf16[256,128]{0,1:T(8,128)(2,1)S(1)}, bf16[256,128]{0,1:T(8,128)(2,1)}, u32[]{:S(2)}, u32[]{:S(2)}) collective-permute-start(bf16[256,128]{0,1:T(8,128)(2,1)S(1)} %copy.60), channel_id=1, source_target_pairs={{0,16},{8,24},{16,32},{24,40},{32,48},{40,56},{48,64},{56,72},{64,... | collective-permute-start | bytes 196616 | tf_op jit(solution)/shard_map/ppermute | solution.py:43
  38.7 1.4 broadcast_in_dim.30
  40.1 4.8 %all-to-all-start.1 = ((bf16[8,256,512]{1,2,0:T(8,128)(2,1)}), bf16[8,256,512]{1,2,0:T(8,128)(2,1)S(1)}, u32[]{:S(2)}, u32[]{:S(2)}) async-start(bf16[8,256,512]{1,2,0:T(8,128)(2,1)} %broadcast_in_dim.30), calls=%async_computation.1 | async-start | bytes 4194304 | tf_op jit(solution)/shard_map/all_to_all | solution.py:33
  48.1 1.4 copy-done.1
  49.5 3.1 %convert_bitcast_fusion = bf16[8,256,768]{1,2,0:T(8,128)(2,1)} fusion(f32[8,256]{1,0:T(8,128)S(1)} %fusion.4, f32[8,256]{1,0:T(8,128)S(1)} %get-tuple-element.24, f32[768,256,8]{1,0,2:T(8,128)S(1)} %get-tuple-element.25, pred[256,768]{0,1:T(8,128)(4,1)S(1)} %compare_and_fusion), kind=kLoop, calls=%fused_computation.11 | loop fusion | flops 7864320 | bytes 9650176 | tf_op jit(solution)/shard_map/reshape.20
  52.6 5.1 %copy.74 = bf16[8,256,768]{2,0,1:T(8,128)(2,1)} copy(bf16[8,256,768]{1,2,0:T(8,128)(2,1)} %convert_bitcast_fusion) | data formatting | bytes 6291456 | tf_op jit(solution)/shard_map/reshape.20
  57.6 11.3 %all-to-all-done.1 = bf16[8,256,512]{1,2,0:T(8,128)(2,1)S(1)} async-done(((bf16[8,256,512]{1,2,0:T(8,128)(2,1)}), bf16[8,256,512]{1,2,0:T(8,128)(2,1)S(1)}, u32[]{:S(2)}, u32[]{:S(2)}) %all-to-all-start.1) | async-done | bytes 2097184 | tf_op jit(solution)/shard_map/all_to_all | solution.py:33
  69.0 59.5 %all-gather.2.cloned.1.call-done = bf16[1024,4096]{1,0:T(8,128)(2,1)} async-done(((bf16[64,4096]{1,0:T(8,128)(2,1)}), bf16[1024,4096]{1,0:T(8,128)(2,1)}) %all-gather.2.cloned.1.call-update) | async-done | bytes 8388624 | tf_op jit(solution)/shard_map/all_gather | solution.py:21
  128.5 5.8 %convolution_convert_fusion.1 = bf16[256,1024]{1,0:T(8,128)(2,1)S(1)} fusion(bf16[256,4096]{0,1:T(8,128)(2,1)S(1)} %bitcast.148, bf16[1024,4096]{1,0:T(8,128)(2,1)} %all-gather.2.cloned.1.call-done), kind=kOutput, calls=%fused_computation.13 | convolution fusion | flops 2147745792 | bytes 11010048 | tf_op jit(solution)/shard_map/tc,rc->tr/dot_general | solution.py:108
  134.5 3.2 %multiply_reduce_fusion = (f32[256,8]{0,1:T(8,128)}, bf16[128,8,256]{2,0,1:T(8,128)(2,1)S(1)}) fusion(f32[256,1,8,128]{0,3,2,1:T(8,128)S(1)} %bitcast.145, bf16[8,256,768]{1,2,0:T(8,128)(2,1)} %convert_bitcast_fusion, bf16[256,128]{0,1:T(8,128)(2,1)S(1)} %copy.60, bf16[256,128]{0,1:T(8,128)(2,1)} %collective-permute-done.1, ...), kind=kOutput, calls=%fused_computation.18 | convolution fusion | flops 404289536 | bytes 4923392 | tf_op jit(solution)/shard_map/grtn,ngd->tgrd/dot_general | solution.py:80
  137.7 5.8 %convolution_convert_fusion = bf16[256,4096]{1,0:T(8,128)(2,1)S(1)} fusion(bf16[256,1024]{0,1:T(8,128)(2,1)S(1)} %bitcast.146, bf16[1024,4096]{1,0:T(8,128)(2,1)} %all-gather.2.cloned.1.call-done), kind=kOutput, calls=%fused_computation.8 | convolution fusion | flops 2148532224 | bytes 11010048 | tf_op jit(solution)/shard_map/dot_general | solution.py:133
  143.4 1.6 copy.104
  145.0 4.8 %all-to-all-start = ((bf16[8,256,512]{2,1,0:T(8,128)(2,1)}), bf16[8,256,512]{2,1,0:T(8,128)(2,1)S(1)}, u32[]{:S(2)}, u32[]{:S(2)}) async-start(bf16[8,256,512]{2,1,0:T(8,128)(2,1)} %bitcast.144), calls=%async_computation | async-start | bytes 4194304 | tf_op jit(solution)/shard_map/all_to_all | solution.py:53
  149.9 3.3 %fusion.25 = (bf16[768,1,128]{0,2,1:T(8,128)(2,1)S(1)}, f32[768,1,128]{0,2,1:T(8,128)}) fusion(bf16[256,8,128]{2,1,0:T(8,128)(2,1)S(1)} %bitcast.150, bf16[8,256,768]{2,0,1:T(8,128)(2,1)} %copy.74), kind=kOutput, calls=%fused_computation.49 | convolution fusion | flops 402751488 | bytes 4259840 | tf_op jit(solution)/shard_map/grtn,tgrd->ngd/dot_general | solution.py:92
  153.8 3.3 %collective-permute-start.7 = (bf16[256,128]{0,1:T(8,128)(2,1)}, bf16[256,128]{0,1:T(8,128)(2,1)}, u32[]{:S(2)}, u32[]{:S(2)}) collective-permute-start(bf16[256,128]{0,1:T(8,128)(2,1)} %get-tuple-element.21), channel_id=1, source_target_pairs={{16,0},{24,8},{32,16},{40,24},{48,32},{56,40},{64,48},{72,56},{80,... | collective-permute-start | bytes 196616 | tf_op jit(solution)/shard_map/ppermute | solution.py:43
  157.2 1.9 %collective-permute-start.6 = (bf16[256,128]{0,1:T(8,128)(2,1)}, bf16[256,128]{0,1:T(8,128)(2,1)}, u32[]{:S(2)}, u32[]{:S(2)}) collective-permute-start(bf16[256,128]{0,1:T(8,128)(2,1)} %get-tuple-element.20), channel_id=1, source_target_pairs={{8,0},{16,8},{24,16},{32,24},{40,32},{48,40},{56,48},{64,56},{72,6... | collective-permute-start | bytes 196616 | tf_op jit(solution)/shard_map/ppermute | solution.py:43
  159.1 4.5 %fusion.6 = bf16[8,256,768]{1,2,0:T(8,128)(2,1)S(1)} fusion(f32[8,256]{1,0:T(8,128)} %bitcast.151, f32[8,256]{1,0:T(8,128)S(1)} %fusion.4, f32[8,256]{1,0:T(8,128)S(1)} %get-tuple-element.24, f32[768,256,8]{1,0,2:T(8,128)} %copy-done.1, pred[256,768]{0,1:T(8,128)(4,1)S(1)} %compare_and_fusion, bf16[256,128]{0,1:T(8,128)(2,1)S(1)} %copy.60, ...), kind=kOutput, calls=%fused_computation.10 | convolution fusion | flops 415825920 | bytes 10379264 | tf_op jit(solution)/shard_map/tgrd,ngd->grtn/dot_general | solution.py:84
  166.9 7.6 %collective-permute-start.5 = (bf16[256,128]{1,0:T(8,128)(2,1)}, bf16[256,128]{1,0:T(8,128)(2,1)S(1)}, u32[]{:S(2)}, u32[]{:S(2)}) collective-permute-start(bf16[256,128]{1,0:T(8,128)(2,1)} %get-tuple-element.23), channel_id=1, source_target_pairs={{16,0},{24,8},{32,16},{40,24},{48,32},{56,40},{64,48},{72,56},{80,... | collective-permute-start | bytes 196616 | tf_op jit(solution)/shard_map/ppermute | solution.py:43
  174.5 2.5 %collective-permute-start.4 = (bf16[256,128]{1,0:T(8,128)(2,1)}, bf16[256,128]{1,0:T(8,128)(2,1)S(1)}, u32[]{:S(2)}, u32[]{:S(2)}) collective-permute-start(bf16[256,128]{1,0:T(8,128)(2,1)} %get-tuple-element.22), channel_id=1, source_target_pairs={{8,0},{16,8},{24,16},{32,24},{40,32},{48,40},{56,48},{64,56},{72,6... | collective-permute-start | bytes 196616 | tf_op jit(solution)/shard_map/ppermute | solution.py:43
  178.7 4.3 %collective-permute-done.4 = bf16[256,128]{1,0:T(8,128)(2,1)S(1)} collective-permute-done((bf16[256,128]{1,0:T(8,128)(2,1)}, bf16[256,128]{1,0:T(8,128)(2,1)S(1)}, u32[]{:S(2)}, u32[]{:S(2)}) %collective-permute-start.4) | collective-permute-done | bytes 65568 | tf_op jit(solution)/shard_map/ppermute | solution.py:43
  (43 shorter events, 12.8 us)
Async XLA Ops:
  7.2 38.4 %copy-start = (bf16[256,1024]{1,0:T(8,128)(2,1)S(1)}, bf16[256,1024]{1,0:T(8,128)(2,1)}, u32[]{:S(2)}) copy-start(bf16[256,1024]{1,0:T(8,128)(2,1)} %param.6) | copy-start | bytes 1572868
  7.2 38.4 %copy-start.2 = (bf16[256,128]{1,0:T(8,128)(2,1)S(1)}, bf16[256,128]{1,0:T(8,128)(2,1)}, u32[]{:S(2)}) copy-start(bf16[256,128]{1,0:T(8,128)(2,1)} %param.7) | copy-start | bytes 196612
  7.2 37.7 %copy-start.5 = (s32[64]{0:T(128)S(1)}, s32[64]{0:T(128)}, u32[]{:S(2)}) copy-start(s32[64]{0:T(128)} %param.11) | copy-start | bytes 772
  7.2 121.3 %all-gather.2.cloned.1.call-start = ((), (), s32[]{:S(2)}) async-start(), calls=%async_computation.2 | async-start | bytes 8912896 | tf_op jit(solution)/shard_map/all_gather | solution.py:21
  21.1 24.5 %collective-permute-start.3 = (bf16[256,128]{1,0:T(8,128)(2,1)}, bf16[256,128]{1,0:T(8,128)(2,1)S(1)}, u32[]{:S(2)}, u32[]{:S(2)}) collective-permute-start(bf16[256,128]{1,0:T(8,128)(2,1)} %param.7), channel_id=1, source_target_pairs={{0,8},{8,16},{16,24},{24,32},{32,40},{40,48},{48,56},{56,64},{64,7... | collective-permute-start | bytes 196616 | tf_op jit(solution)/shard_map/ppermute | solution.py:43
  26.0 19.6 %collective-permute-start.2 = (bf16[256,128]{1,0:T(8,128)(2,1)}, bf16[256,128]{1,0:T(8,128)(2,1)S(1)}, u32[]{:S(2)}, u32[]{:S(2)}) collective-permute-start(bf16[256,128]{1,0:T(8,128)(2,1)} %param.7), channel_id=1, source_target_pairs={{0,16},{8,24},{16,32},{24,40},{32,48},{40,56},{48,64},{56,72},{64,... | collective-permute-start | bytes 196616 | tf_op jit(solution)/shard_map/ppermute | solution.py:43
  29.7 104.8 %collective-permute-start.1 = (bf16[256,128]{0,1:T(8,128)(2,1)S(1)}, bf16[256,128]{0,1:T(8,128)(2,1)}, u32[]{:S(2)}, u32[]{:S(2)}) collective-permute-start(bf16[256,128]{0,1:T(8,128)(2,1)S(1)} %copy.60), channel_id=1, source_target_pairs={{0,8},{8,16},{16,24},{24,32},{32,40},{40,48},{48,56},{56,64},{64,7... | collective-permute-start | bytes 196616 | tf_op jit(solution)/shard_map/ppermute | solution.py:43
  33.9 100.6 %collective-permute-start = (bf16[256,128]{0,1:T(8,128)(2,1)S(1)}, bf16[256,128]{0,1:T(8,128)(2,1)}, u32[]{:S(2)}, u32[]{:S(2)}) collective-permute-start(bf16[256,128]{0,1:T(8,128)(2,1)S(1)} %copy.60), channel_id=1, source_target_pairs={{0,16},{8,24},{16,32},{24,40},{32,48},{40,56},{48,64},{56,72},{64,... | collective-permute-start | bytes 196616 | tf_op jit(solution)/shard_map/ppermute | solution.py:43
  40.1 28.8 %all-to-all-start.1 = ((bf16[8,256,512]{1,2,0:T(8,128)(2,1)}), bf16[8,256,512]{1,2,0:T(8,128)(2,1)S(1)}, u32[]{:S(2)}, u32[]{:S(2)}) async-start(bf16[8,256,512]{1,2,0:T(8,128)(2,1)} %broadcast_in_dim.30), calls=%async_computation.1 | async-start | bytes 4194304 | tf_op jit(solution)/shard_map/all_to_all | solution.py:33
  45.6 2.4 %copy-start.3 = (bf16[256,128]{1,0:T(8,128)(2,1)}, bf16[256,128]{1,0:T(8,128)(2,1)S(1)}, u32[]{:S(2)}) copy-start(bf16[256,128]{1,0:T(8,128)(2,1)S(1)} %collective-permute-done.2) | copy-start | bytes 196612
  46.8 2.7 %copy-start.1 = (f32[768,256,8]{1,0,2:T(8,128)}, f32[768,256,8]{1,0,2:T(8,128)S(1)}, u32[]{:S(2)}) copy-start(f32[768,256,8]{1,0,2:T(8,128)S(1)} %get-tuple-element.25) | copy-start | bytes 18874372
  145.0 38.7 %all-to-all-start = ((bf16[8,256,512]{2,1,0:T(8,128)(2,1)}), bf16[8,256,512]{2,1,0:T(8,128)(2,1)S(1)}, u32[]{:S(2)}, u32[]{:S(2)}) async-start(bf16[8,256,512]{2,1,0:T(8,128)(2,1)} %bitcast.144), calls=%async_computation | async-start | bytes 4194304 | tf_op jit(solution)/shard_map/all_to_all | solution.py:53
  153.8 23.1 %collective-permute-start.7 = (bf16[256,128]{0,1:T(8,128)(2,1)}, bf16[256,128]{0,1:T(8,128)(2,1)}, u32[]{:S(2)}, u32[]{:S(2)}) collective-permute-start(bf16[256,128]{0,1:T(8,128)(2,1)} %get-tuple-element.21), channel_id=1, source_target_pairs={{16,0},{24,8},{32,16},{40,24},{48,32},{56,40},{64,48},{72,56},{80,... | collective-permute-start | bytes 196616 | tf_op jit(solution)/shard_map/ppermute | solution.py:43
  157.2 19.8 %collective-permute-start.6 = (bf16[256,128]{0,1:T(8,128)(2,1)}, bf16[256,128]{0,1:T(8,128)(2,1)}, u32[]{:S(2)}, u32[]{:S(2)}) collective-permute-start(bf16[256,128]{0,1:T(8,128)(2,1)} %get-tuple-element.20), channel_id=1, source_target_pairs={{8,0},{16,8},{24,16},{32,24},{40,32},{48,40},{56,48},{64,56},{72,6... | collective-permute-start | bytes 196616 | tf_op jit(solution)/shard_map/ppermute | solution.py:43
  159.1 4.5 %copy-start.4 = (bf16[256,128]{1,0:T(8,128)(2,1)S(1)}, bf16[256,128]{1,0:T(8,128)(2,1)}, u32[]{:S(2)}) copy-start(bf16[256,128]{1,0:T(8,128)(2,1)} %copy-done.3) | copy-start | bytes 196612
  166.9 11.8 %collective-permute-start.5 = (bf16[256,128]{1,0:T(8,128)(2,1)}, bf16[256,128]{1,0:T(8,128)(2,1)S(1)}, u32[]{:S(2)}, u32[]{:S(2)}) collective-permute-start(bf16[256,128]{1,0:T(8,128)(2,1)} %get-tuple-element.23), channel_id=1, source_target_pairs={{16,0},{24,8},{32,16},{40,24},{48,32},{56,40},{64,48},{72,56},{80,... | collective-permute-start | bytes 196616 | tf_op jit(solution)/shard_map/ppermute | solution.py:43
  174.5 8.5 %collective-permute-start.4 = (bf16[256,128]{1,0:T(8,128)(2,1)}, bf16[256,128]{1,0:T(8,128)(2,1)S(1)}, u32[]{:S(2)}, u32[]{:S(2)}) collective-permute-start(bf16[256,128]{1,0:T(8,128)(2,1)} %get-tuple-element.22), channel_id=1, source_target_pairs={{8,0},{16,8},{24,16},{32,24},{40,32},{48,40},{56,48},{64,56},{72,6... | collective-permute-start | bytes 196616 | tf_op jit(solution)/shard_map/ppermute | solution.py:43
Sparse Core Ops, SparseCore 0:
  21.3 107.1 all-gather.1
where the time goes:
time: 192 us
  waiting for transfers between devices  75.2 us (39%)
  starting transfers between devices  40.4 us (21%)
  matrix products  25.2 us (13%)
  local copies, waits for them, and re-layouts  15 us (8%)
  between operations  14.3 us (7%)
  blocking collectives  13.9 us (7%)
  other arithmetic  7.6 us (4%)
    all_gather x1, waiting for transfers between devices, gather_axes(): filled = lax.all_gather(filled, axes[number], axis=dim, tiled=True)  59.5 us
    ppermute x8, starting transfers between devices, passed_along(): return lax.ppermute(block, axis, route)  30.8 us
    all_gather x1, blocking collectives, gather_axes(): filled = lax.all_gather(filled, axes[number], axis=dim, tiled=True)  13.9 us
    all_to_all x1, waiting for transfers between devices, from_everyone(): lax.all_to_all(jnp.broadcast_to(x[None], (size, *x.shape)), axis, 0, 0, t...  11.3 us
    dot_general x1, matrix products, on_device(): jnp.einsum('tc,rc->tr', upstream_all, group_weight, preferred_element_typ...  5.76 us
    dot_general x1, matrix products, on_device(): jnp.dot(attended, group_weight, preferred_element_type=jnp.float32)  5.75 us
    unnamed x17, local copies, waits for them, and re-layouts  5.26 us
    another operation x2, local copies, waits for them, and re-layouts  5.16 us
  transfers between devices with their start and end apart: 11, of which 3 were waited for; matrix products, arithmetic and copies ran while one was open for 18% of the time, Pallas kernels for 0%

commit v1 on v0

--- a/solution.py
+++ b/solution.py
@@ -103,7 +103,7 @@
 def on_device(queries, keys, values, output_grad, out_weight, lengths):
     block_rows = queries.shape[0]
     device = lax.axis_index(DP)
-    group_weight = gather_axes(out_weight, DP, 0)
+    group_weight = lax.all_gather(out_weight, DP, axis=0, tiled=True)
     upstream_all = gather_directly(output_grad, "head", 1)
     d_attended = jnp.einsum(
         "tc,rc->tr", upstream_all, group_weight, preferred_element_type=jnp.float32

time: 192 us -> 231 us (1.20)
  waiting for transfers between devices: 75.2 us -> 130 us
  blocking collectives: 13.9 us -> 0 us
    all_gather x1, waiting for transfers between devices: 59.5 us -> 113 us  [on_device(): group_weight = lax.all_gather(out_weight, DP, axis=0, tiled=True)]
    all_gather x1 -> x0, blocking collectives: 13.9 us -> none  [gather_axes(): filled = lax.all_gather(filled, axes[number], axis=dim, tiled=True)]
  transfers between devices with their start and end apart: 11 -> 11, of which waited for: 3 -> 4; matrix products, arithmetic and copies ran while one was open for 18% -> 15% of each run, Pallas kernels for 0% -> 0%
where the time goes in v1:
time: 231 us; the launch traced here: 230 us
  waiting for transfers between devices  130 us (56%)
  starting transfers between devices  38.6 us (17%)
  matrix products  25.2 us (11%)
  local copies, waits for them, and re-layouts  15 us (6%)
  between operations  14.3 us (6%)
  other arithmetic  7.6 us (3%)
    all_gather x1, waiting for transfers between devices, on_device(): group_weight = lax.all_gather(out_weight, DP, axis=0, tiled=True)  113 us
    ppermute x8, starting transfers between devices, passed_along(): return lax.ppermute(block, axis, route)  28.9 us
    all_to_all x1, waiting for transfers between devices, from_everyone(): lax.all_to_all(jnp.broadcast_to(x[None], (size, *x.shape)), axis, 0, 0, t...  11.3 us
    dot_general x1, matrix products, on_device(): jnp.einsum('tc,rc->tr', upstream_all, group_weight, preferred_element_typ...  5.76 us
    dot_general x1, matrix products, on_device(): jnp.dot(attended, group_weight, preferred_element_type=jnp.float32)  5.75 us
    unnamed x17, local copies, waits for them, and re-layouts  5.25 us
    another operation x2, local copies, waits for them, and re-layouts  5.16 us
    all_to_all x1, starting transfers between devices, sent_and_summed(): lax.all_to_all(pieces, axis, split_axis=0, concat_axis=0, tiled=True)  4.8 us
  transfers between devices with their start and end apart: 11, of which 4 were waited for; matrix products, arithmetic and copies ran while one was open for 15% of the time, Pallas kernels for 0%

profile of v1, /device:TPU:54, one launch (start us, length us, event | category | flops | bytes accessed | tf_op | source)
XLA Modules:
  0.0 230.1 jit_solution(14787751482215236873)
XLA Ops:
  7.9 3.7 %collective-permute-start.3 = (bf16[256,128]{1,0:T(8,128)(2,1)}, bf16[256,128]{1,0:T(8,128)(2,1)S(1)}, u32[]{:S(2)}, u32[]{:S(2)}) collective-permute-start(bf16[256,128]{1,0:T(8,128)(2,1)} %param.7), channel_id=1, source_target_pairs={{0,8},{8,16},{16,24},{24,32},{32,40},{40,48},{48,56},{56,64},{64,7... | collective-permute-start | bytes 196616 | tf_op jit(solution)/shard_map/ppermute | solution.py:43
  11.7 4.3 %collective-permute-start.2 = (bf16[256,128]{1,0:T(8,128)(2,1)}, bf16[256,128]{1,0:T(8,128)(2,1)S(1)}, u32[]{:S(2)}, u32[]{:S(2)}) collective-permute-start(bf16[256,128]{1,0:T(8,128)(2,1)} %param.7), channel_id=1, source_target_pairs={{0,16},{8,24},{16,32},{24,40},{32,48},{40,56},{48,64},{56,72},{64,... | collective-permute-start | bytes 196616 | tf_op jit(solution)/shard_map/ppermute | solution.py:43
  17.0 3.7 %collective-permute-start.1 = (bf16[256,128]{0,1:T(8,128)(2,1)S(1)}, bf16[256,128]{0,1:T(8,128)(2,1)}, u32[]{:S(2)}, u32[]{:S(2)}) collective-permute-start(bf16[256,128]{0,1:T(8,128)(2,1)S(1)} %copy.60), channel_id=1, source_target_pairs={{0,8},{8,16},{16,24},{24,32},{32,40},{40,48},{48,56},{56,64},{64,7... | collective-permute-start | bytes 196616 | tf_op jit(solution)/shard_map/ppermute | solution.py:43
  20.7 3.5 %collective-permute-start = (bf16[256,128]{0,1:T(8,128)(2,1)S(1)}, bf16[256,128]{0,1:T(8,128)(2,1)}, u32[]{:S(2)}, u32[]{:S(2)}) collective-permute-start(bf16[256,128]{0,1:T(8,128)(2,1)S(1)} %copy.60), channel_id=1, source_target_pairs={{0,16},{8,24},{16,32},{24,40},{32,48},{40,56},{48,64},{56,72},{64,... | collective-permute-start | bytes 196616 | tf_op jit(solution)/shard_map/ppermute | solution.py:43
  25.2 1.4 broadcast_in_dim.30
  26.7 4.8 %all-to-all-start.1 = ((bf16[8,256,512]{1,2,0:T(8,128)(2,1)}), bf16[8,256,512]{1,2,0:T(8,128)(2,1)S(1)}, u32[]{:S(2)}, u32[]{:S(2)}) async-start(bf16[8,256,512]{1,2,0:T(8,128)(2,1)} %broadcast_in_dim.30), calls=%async_computation.1 | async-start | bytes 4194304 | tf_op jit(solution)/shard_map/all_to_all | solution.py:33
  33.3 1.3 fusion.4
  34.7 1.4 copy-done.1
  36.0 3.1 %convert_bitcast_fusion = bf16[8,256,768]{1,2,0:T(8,128)(2,1)} fusion(f32[8,256]{1,0:T(8,128)S(1)} %fusion.4, f32[8,256]{1,0:T(8,128)S(1)} %get-tuple-element.24, f32[768,256,8]{1,0,2:T(8,128)S(1)} %get-tuple-element.25, pred[256,768]{0,1:T(8,128)(4,1)S(1)} %compare_and_fusion), kind=kLoop, calls=%fused_computation.11 | loop fusion | flops 7864320 | bytes 9650176 | tf_op jit(solution)/shard_map/reshape.20
  39.1 5.1 %copy.74 = bf16[8,256,768]{2,0,1:T(8,128)(2,1)} copy(bf16[8,256,768]{1,2,0:T(8,128)(2,1)} %convert_bitcast_fusion) | data formatting | bytes 6291456 | tf_op jit(solution)/shard_map/reshape.20
  44.2 11.3 %all-to-all-done.1 = bf16[8,256,512]{1,2,0:T(8,128)(2,1)S(1)} async-done(((bf16[8,256,512]{1,2,0:T(8,128)(2,1)}), bf16[8,256,512]{1,2,0:T(8,128)(2,1)S(1)}, u32[]{:S(2)}, u32[]{:S(2)}) %all-to-all-start.1) | async-done | bytes 2097184 | tf_op jit(solution)/shard_map/all_to_all | solution.py:33
  55.5 113.4 %all-gather.2.cloned.1.call-done = bf16[1024,4096]{1,0:T(8,128)(2,1)} async-done(((bf16[16,4096]{1,0:T(8,128)(2,1)}), bf16[1024,4096]{1,0:T(8,128)(2,1)}) %all-gather.2.cloned.1.call-update) | async-done | bytes 8388624 | tf_op jit(solution)/shard_map/all_gather | solution.py:106
  169.0 5.8 %convolution_convert_fusion.1 = bf16[256,1024]{1,0:T(8,128)(2,1)S(1)} fusion(bf16[256,4096]{0,1:T(8,128)(2,1)S(1)} %bitcast.148, bf16[1024,4096]{1,0:T(8,128)(2,1)} %all-gather.2.cloned.1.call-done), kind=kOutput, calls=%fused_computation.13 | convolution fusion | flops 2147745792 | bytes 11010048 | tf_op jit(solution)/shard_map/tc,rc->tr/dot_general | solution.py:108
  175.0 3.2 %multiply_reduce_fusion = (f32[256,8]{0,1:T(8,128)}, bf16[128,8,256]{2,0,1:T(8,128)(2,1)S(1)}) fusion(f32[256,1,8,128]{0,3,2,1:T(8,128)S(1)} %bitcast.145, bf16[8,256,768]{1,2,0:T(8,128)(2,1)} %convert_bitcast_fusion, bf16[256,128]{0,1:T(8,128)(2,1)S(1)} %copy.60, bf16[256,128]{0,1:T(8,128)(2,1)} %collective-permute-done.1, ...), kind=kOutput, calls=%fused_computation.18 | convolution fusion | flops 404289536 | bytes 4923392 | tf_op jit(solution)/shard_map/grtn,ngd->tgrd/dot_general | solution.py:80
  178.1 5.8 %convolution_convert_fusion = bf16[256,4096]{1,0:T(8,128)(2,1)S(1)} fusion(bf16[256,1024]{0,1:T(8,128)(2,1)S(1)} %bitcast.146, bf16[1024,4096]{1,0:T(8,128)(2,1)} %all-gather.2.cloned.1.call-done), kind=kOutput, calls=%fused_computation.8 | convolution fusion | flops 2148532224 | bytes 11010048 | tf_op jit(solution)/shard_map/dot_general | solution.py:133
  183.9 1.6 copy.104
  185.4 4.8 %all-to-all-start = ((bf16[8,256,512]{2,1,0:T(8,128)(2,1)}), bf16[8,256,512]{2,1,0:T(8,128)(2,1)S(1)}, u32[]{:S(2)}, u32[]{:S(2)}) async-start(bf16[8,256,512]{2,1,0:T(8,128)(2,1)} %bitcast.144), calls=%async_computation | async-start | bytes 4194304 | tf_op jit(solution)/shard_map/all_to_all | solution.py:53
  190.4 3.3 %fusion.25 = (bf16[768,1,128]{0,2,1:T(8,128)(2,1)S(1)}, f32[768,1,128]{0,2,1:T(8,128)}) fusion(bf16[256,8,128]{2,1,0:T(8,128)(2,1)S(1)} %bitcast.150, bf16[8,256,768]{2,0,1:T(8,128)(2,1)} %copy.74), kind=kOutput, calls=%fused_computation.49 | convolution fusion | flops 402751488 | bytes 4259840 | tf_op jit(solution)/shard_map/grtn,tgrd->ngd/dot_general | solution.py:92
  194.3 3.7 %collective-permute-start.7 = (bf16[256,128]{0,1:T(8,128)(2,1)}, bf16[256,128]{0,1:T(8,128)(2,1)}, u32[]{:S(2)}, u32[]{:S(2)}) collective-permute-start(bf16[256,128]{0,1:T(8,128)(2,1)} %get-tuple-element.21), channel_id=1, source_target_pairs={{16,0},{24,8},{32,16},{40,24},{48,32},{56,40},{64,48},{72,56},{80,... | collective-permute-start | bytes 196616 | tf_op jit(solution)/shard_map/ppermute | solution.py:43
  198.1 3.3 %collective-permute-start.6 = (bf16[256,128]{0,1:T(8,128)(2,1)}, bf16[256,128]{0,1:T(8,128)(2,1)}, u32[]{:S(2)}, u32[]{:S(2)}) collective-permute-start(bf16[256,128]{0,1:T(8,128)(2,1)} %get-tuple-element.20), channel_id=1, source_target_pairs={{8,0},{16,8},{24,16},{32,24},{40,32},{48,40},{56,48},{64,56},{72,6... | collective-permute-start | bytes 196616 | tf_op jit(solution)/shard_map/ppermute | solution.py:43
  201.4 4.5 %fusion.6 = bf16[8,256,768]{1,2,0:T(8,128)(2,1)S(1)} fusion(f32[8,256]{1,0:T(8,128)} %bitcast.151, f32[8,256]{1,0:T(8,128)S(1)} %fusion.4, f32[8,256]{1,0:T(8,128)S(1)} %get-tuple-element.24, f32[768,256,8]{1,0,2:T(8,128)} %copy-done.1, pred[256,768]{0,1:T(8,128)(4,1)S(1)} %compare_and_fusion, bf16[256,128]{0,1:T(8,128)(2,1)S(1)} %copy.60, ...), kind=kOutput, calls=%fused_computation.10 | convolution fusion | flops 415825920 | bytes 10379264 | tf_op jit(solution)/shard_map/tgrd,ngd->grtn/dot_general | solution.py:84
  209.2 3.9 %collective-permute-start.5 = (bf16[256,128]{1,0:T(8,128)(2,1)}, bf16[256,128]{1,0:T(8,128)(2,1)S(1)}, u32[]{:S(2)}, u32[]{:S(2)}) collective-permute-start(bf16[256,128]{1,0:T(8,128)(2,1)} %get-tuple-element.23), channel_id=1, source_target_pairs={{16,0},{24,8},{32,16},{40,24},{48,32},{56,40},{64,48},{72,56},{80,... | collective-permute-start | bytes 196616 | tf_op jit(solution)/shard_map/ppermute | solution.py:43
  213.1 2.7 %collective-permute-start.4 = (bf16[256,128]{1,0:T(8,128)(2,1)}, bf16[256,128]{1,0:T(8,128)(2,1)S(1)}, u32[]{:S(2)}, u32[]{:S(2)}) collective-permute-start(bf16[256,128]{1,0:T(8,128)(2,1)} %get-tuple-element.22), channel_id=1, source_target_pairs={{8,0},{16,8},{24,16},{32,24},{40,32},{48,40},{56,48},{64,56},{72,6... | collective-permute-start | bytes 196616 | tf_op jit(solution)/shard_map/ppermute | solution.py:43
  218.0 3.6 %collective-permute-done.4 = bf16[256,128]{1,0:T(8,128)(2,1)S(1)} collective-permute-done((bf16[256,128]{1,0:T(8,128)(2,1)}, bf16[256,128]{1,0:T(8,128)(2,1)S(1)}, u32[]{:S(2)}, u32[]{:S(2)}) %collective-permute-start.4) | collective-permute-done | bytes 65568 | tf_op jit(solution)/shard_map/ppermute | solution.py:43
  (42 shorter events, 12.6 us)
Async XLA Ops:
  7.2 25.0 %copy-start = (bf16[256,1024]{1,0:T(8,128)(2,1)S(1)}, bf16[256,1024]{1,0:T(8,128)(2,1)}, u32[]{:S(2)}) copy-start(bf16[256,1024]{1,0:T(8,128)(2,1)} %param.6) | copy-start | bytes 1572868
  7.2 25.0 %copy-start.2 = (bf16[256,128]{1,0:T(8,128)(2,1)S(1)}, bf16[256,128]{1,0:T(8,128)(2,1)}, u32[]{:S(2)}) copy-start(bf16[256,128]{1,0:T(8,128)(2,1)} %param.7) | copy-start | bytes 196612
  7.2 24.3 %copy-start.5 = (s32[64]{0:T(128)S(1)}, s32[64]{0:T(128)}, u32[]{:S(2)}) copy-start(s32[64]{0:T(128)} %param.11) | copy-start | bytes 772
  7.2 161.8 %all-gather.2.cloned.1.call-start = ((), (), s32[]{:S(2)}) async-start(), calls=%async_computation.2 | async-start | bytes 8519680 | tf_op jit(solution)/shard_map/all_gather | solution.py:106
  7.9 24.2 %collective-permute-start.3 = (bf16[256,128]{1,0:T(8,128)(2,1)}, bf16[256,128]{1,0:T(8,128)(2,1)S(1)}, u32[]{:S(2)}, u32[]{:S(2)}) collective-permute-start(bf16[256,128]{1,0:T(8,128)(2,1)} %param.7), channel_id=1, source_target_pairs={{0,8},{8,16},{16,24},{24,32},{32,40},{40,48},{48,56},{56,64},{64,7... | collective-permute-start | bytes 196616 | tf_op jit(solution)/shard_map/ppermute | solution.py:43
  11.7 20.5 %collective-permute-start.2 = (bf16[256,128]{1,0:T(8,128)(2,1)}, bf16[256,128]{1,0:T(8,128)(2,1)S(1)}, u32[]{:S(2)}, u32[]{:S(2)}) collective-permute-start(bf16[256,128]{1,0:T(8,128)(2,1)} %param.7), channel_id=1, source_target_pairs={{0,16},{8,24},{16,32},{24,40},{32,48},{40,56},{48,64},{56,72},{64,... | collective-permute-start | bytes 196616 | tf_op jit(solution)/shard_map/ppermute | solution.py:43
  17.0 158.0 %collective-permute-start.1 = (bf16[256,128]{0,1:T(8,128)(2,1)S(1)}, bf16[256,128]{0,1:T(8,128)(2,1)}, u32[]{:S(2)}, u32[]{:S(2)}) collective-permute-start(bf16[256,128]{0,1:T(8,128)(2,1)S(1)} %copy.60), channel_id=1, source_target_pairs={{0,8},{8,16},{16,24},{24,32},{32,40},{40,48},{48,56},{56,64},{64,7... | collective-permute-start | bytes 196616 | tf_op jit(solution)/shard_map/ppermute | solution.py:43
  20.7 154.3 %collective-permute-start = (bf16[256,128]{0,1:T(8,128)(2,1)S(1)}, bf16[256,128]{0,1:T(8,128)(2,1)}, u32[]{:S(2)}, u32[]{:S(2)}) collective-permute-start(bf16[256,128]{0,1:T(8,128)(2,1)S(1)} %copy.60), channel_id=1, source_target_pairs={{0,16},{8,24},{16,32},{24,40},{32,48},{40,56},{48,64},{56,72},{64,... | collective-permute-start | bytes 196616 | tf_op jit(solution)/shard_map/ppermute | solution.py:43
  26.7 28.8 %all-to-all-start.1 = ((bf16[8,256,512]{1,2,0:T(8,128)(2,1)}), bf16[8,256,512]{1,2,0:T(8,128)(2,1)S(1)}, u32[]{:S(2)}, u32[]{:S(2)}) async-start(bf16[8,256,512]{1,2,0:T(8,128)(2,1)} %broadcast_in_dim.30), calls=%async_computation.1 | async-start | bytes 4194304 | tf_op jit(solution)/shard_map/all_to_all | solution.py:33
  32.2 2.4 %copy-start.3 = (bf16[256,128]{1,0:T(8,128)(2,1)}, bf16[256,128]{1,0:T(8,128)(2,1)S(1)}, u32[]{:S(2)}) copy-start(bf16[256,128]{1,0:T(8,128)(2,1)S(1)} %collective-permute-done.2) | copy-start | bytes 196612
  33.3 2.7 %copy-start.1 = (f32[768,256,8]{1,0,2:T(8,128)}, f32[768,256,8]{1,0,2:T(8,128)S(1)}, u32[]{:S(2)}) copy-start(f32[768,256,8]{1,0,2:T(8,128)S(1)} %get-tuple-element.25) | copy-start | bytes 18874372
  185.4 36.8 %all-to-all-start = ((bf16[8,256,512]{2,1,0:T(8,128)(2,1)}), bf16[8,256,512]{2,1,0:T(8,128)(2,1)S(1)}, u32[]{:S(2)}, u32[]{:S(2)}) async-start(bf16[8,256,512]{2,1,0:T(8,128)(2,1)} %bitcast.144), calls=%async_computation | async-start | bytes 4194304 | tf_op jit(solution)/shard_map/all_to_all | solution.py:53
  194.3 21.5 %collective-permute-start.7 = (bf16[256,128]{0,1:T(8,128)(2,1)}, bf16[256,128]{0,1:T(8,128)(2,1)}, u32[]{:S(2)}, u32[]{:S(2)}) collective-permute-start(bf16[256,128]{0,1:T(8,128)(2,1)} %get-tuple-element.21), channel_id=1, source_target_pairs={{16,0},{24,8},{32,16},{40,24},{48,32},{56,40},{64,48},{72,56},{80,... | collective-permute-start | bytes 196616 | tf_op jit(solution)/shard_map/ppermute | solution.py:43
  198.1 17.8 %collective-permute-start.6 = (bf16[256,128]{0,1:T(8,128)(2,1)}, bf16[256,128]{0,1:T(8,128)(2,1)}, u32[]{:S(2)}, u32[]{:S(2)}) collective-permute-start(bf16[256,128]{0,1:T(8,128)(2,1)} %get-tuple-element.20), channel_id=1, source_target_pairs={{8,0},{16,8},{24,16},{32,24},{40,32},{48,40},{56,48},{64,56},{72,6... | collective-permute-start | bytes 196616 | tf_op jit(solution)/shard_map/ppermute | solution.py:43
  201.4 4.5 %copy-start.4 = (bf16[256,128]{1,0:T(8,128)(2,1)S(1)}, bf16[256,128]{1,0:T(8,128)(2,1)}, u32[]{:S(2)}) copy-start(bf16[256,128]{1,0:T(8,128)(2,1)} %copy-done.3) | copy-start | bytes 196612
  209.2 8.8 %collective-permute-start.5 = (bf16[256,128]{1,0:T(8,128)(2,1)}, bf16[256,128]{1,0:T(8,128)(2,1)S(1)}, u32[]{:S(2)}, u32[]{:S(2)}) collective-permute-start(bf16[256,128]{1,0:T(8,128)(2,1)} %get-tuple-element.23), channel_id=1, source_target_pairs={{16,0},{24,8},{32,16},{40,24},{48,32},{56,40},{64,48},{72,56},{80,... | collective-permute-start | bytes 196616 | tf_op jit(solution)/shard_map/ppermute | solution.py:43
  213.1 8.5 %collective-permute-start.4 = (bf16[256,128]{1,0:T(8,128)(2,1)}, bf16[256,128]{1,0:T(8,128)(2,1)S(1)}, u32[]{:S(2)}, u32[]{:S(2)}) collective-permute-start(bf16[256,128]{1,0:T(8,128)(2,1)} %get-tuple-element.22), channel_id=1, source_target_pairs={{8,0},{16,8},{24,16},{32,24},{40,32},{48,40},{56,48},{64,56},{72,6... | collective-permute-start | bytes 196616 | tf_op jit(solution)/shard_map/ppermute | solution.py:43
Sparse Core Ops, SparseCore 0:
  11.0 157.9 all-gather.1

commit v2 on v1

v2 whole, which is shorter than its diff:
```python
import functools
import math

import jax
import jax.numpy as jnp
from jax import lax
from jax.experimental import pallas as pl
from jax.experimental.pallas import tpu as pltpu
from jax.sharding import Mesh
from jax.sharding import PartitionSpec as P

HD=128
LOG2E=1.4426950408889634
NT=(((1,),(1,)),((),()))

def dot_nt(a,b):
    return lax.dot_general(a,b,NT,preferred_element_type=jnp.float32)
def dot_nn(a,b):
    return jnp.dot(a,b,preferred_element_type=jnp.float32)

def forward_body(scaling, group, lengths, place, q, k2, k1, k0, v2, v1, v0, att, shares, bias, vt):
    rows = q.shape[0]
    blocks = 3
    @pl.when(pl.program_id(0) == 0)
    def _():
        first = place[0] * rows
        at = first + lax.broadcasted_iota(jnp.int32, (1, rows), 1)
        def doc(d, carry):
            end, start = carry
            end = end + lengths[d]
            return end, jnp.where(end <= at, end, start)
        _, start = lax.fori_loop(0, lengths.shape[0], doc, (jnp.int32(0), jnp.zeros((1, rows), jnp.int32)))
        keyed = first - (blocks - 1) * rows + lax.broadcasted_iota(jnp.int32, (blocks * rows, rows), 0)
        bias[...] = jnp.where((keyed >= start) & (keyed <= at), 0.0, -1e30)
        for j, v in enumerate((v2, v1, v0)):
            vt[:, j * rows:(j + 1) * rows] = v[...].T
    for h in range(group):
        cols = slice(h * HD, (h + 1) * HD)
        qh = q[:, cols]
        s = [dot_nt(k[...], qh) * (scaling * LOG2E) + bias[j * rows:(j + 1) * rows, :] for j, k in enumerate((k2, k1, k0))]
        top = functools.reduce(jnp.maximum, [jnp.max(x, axis=0, keepdims=True) for x in s])
        e = [jnp.exp2(x - top) for x in s]
        inv = 1.0 / sum(jnp.sum(x, axis=0, keepdims=True) for x in e)
        out = jnp.zeros((HD, rows), jnp.float32)
        for j, x in enumerate(e):
            p = (x * inv).astype(jnp.bfloat16)
            shares[h, j * rows:(j + 1) * rows, :] = p
            out = out + dot_nn(vt[:, j * rows:(j + 1) * rows], p)
        att[:, cols] = out.T.astype(jnp.bfloat16)

def forward(lengths, place, q, ks, vs, group=2):
    rows, width = q.shape
    heads = width // HD
    whole = pl.BlockSpec((rows, HD), lambda i: (0, 0))
    smem = pl.BlockSpec(memory_space=pltpu.SMEM)
    return pl.pallas_call(
        functools.partial(forward_body, 1.0 / math.sqrt(HD), group),
        grid=(heads // group,),
        in_specs=[smem, smem, pl.BlockSpec((rows, group * HD), lambda i: (0, i))] + [whole] * 6,
        out_specs=[pl.BlockSpec((rows, group * HD), lambda i: (0, i)),
                   pl.BlockSpec((group, 3 * rows, rows), lambda i: (i, 0, 0))],
        out_shape=[jax.ShapeDtypeStruct((rows, width), jnp.bfloat16),
                   jax.ShapeDtypeStruct((heads, 3 * rows, rows), jnp.bfloat16)],
        scratch_shapes=[pltpu.VMEM((3 * rows, rows), jnp.float32), pltpu.VMEM((HD, 3 * rows), jnp.bfloat16)],
        compiler_params=pltpu.CompilerParams(dimension_semantics=("arbitrary",)),
        name="attend_forward",
    )(lengths, place, q, *ks, *vs)

def backward_body(scaling, group, parts, *refs):
    (q, k2, k1, k0, v2, v1, v0, da_parts, att, shares, dq, dk2, dk1, dk0, dv2, dv1, dv0, kt, dka, dva) = refs
    rows = q.shape[0]
    step = pl.program_id(0)
    @pl.when(step == 0)
    def _():
        for j, k in enumerate((k2, k1, k0)):
            kt[:, j * rows:(j + 1) * rows] = k[...].T
        dka[...] = jnp.zeros_like(dka)
        dva[...] = jnp.zeros_like(dva)
    for h in range(group):
        cols = slice(h * HD, (h + 1) * HD)
        qh = q[:, cols]
        da = sum(da_parts[i, :, cols].astype(jnp.float32) for i in range(parts)).astype(jnp.bfloat16)
        prod = da.astype(jnp.float32) * att[:, cols].astype(jnp.float32)
        dots = jnp.sum(prod.T, axis=0, keepdims=True)
        out = jnp.zeros((HD, rows), jnp.float32)
        for j, v in enumerate((v2, v1, v0)):
            own = slice(j * rows, (j + 1) * rows)
            p = shares[h, own, :]
            d = dot_nt(v[...], da)
            ds = (p.astype(jnp.float32) * (d - dots)).astype(jnp.bfloat16)
            out = out + dot_nn(kt[:, own], ds)
            dka[own, :] += dot_nn(ds, qh)
            dva[own, :] += dot_nn(p, da)
        dq[:, cols] = (out.T * scaling).astype(jnp.bfloat16)
    @pl.when(step == pl.num_programs(0) - 1)
    def _():
        for j, (dk, dv) in enumerate(((dk2, dv2), (dk1, dv1), (dk0, dv0))):
            own = slice(j * rows, (j + 1) * rows)
            dk[...] = (dka[own, :] * scaling).astype(dk.dtype)
            dv[...] = dva[own, :].astype(dv.dtype)

def backward(q, ks, vs, da_parts, att, shares, group=2):
    rows, width = q.shape
    heads = width // HD
    parts = da_parts.shape[0]
    whole = pl.BlockSpec((rows, HD), lambda i: (0, 0))
    head = pl.BlockSpec((rows, group * HD), lambda i: (0, i))
    piece = lambda t: jax.ShapeDtypeStruct((rows, HD), t)
    bf, f32 = jnp.bfloat16, jnp.float32
    return pl.pallas_call(
        functools.partial(backward_body, 1.0 / math.sqrt(HD), group, parts),
        grid=(heads // group,),
        in_specs=[head] + [whole] * 6 + [pl.BlockSpec((parts, rows, group * HD), lambda i: (0, 0, i)), head,
                  pl.BlockSpec((group, 3 * rows, rows), lambda i: (i, 0, 0))],
        out_specs=[head] + [whole] * 6,
        out_shape=[jax.ShapeDtypeStruct((rows, width), bf)] + [piece(bf), piece(bf), piece(f32)] * 2,
        scratch_shapes=[pltpu.VMEM((HD, 3 * rows), bf), pltpu.VMEM((3 * rows, HD), f32), pltpu.VMEM((3 * rows, HD), f32)],
        compiler_params=pltpu.CompilerParams(dimension_semantics=("arbitrary",)),
        name="attend_backward",
    )(q, *ks, *vs, da_parts, att, shares)

def back_body(og, w, out, lhs):
    @pl.when(pl.program_id(0) == 0)
    def _():
        for h in range(og.shape[0]):
            lhs[:, h * HD:(h + 1) * HD] = og[h]
    out[...] = dot_nt(lhs[...], w[...]).astype(out.dtype)


def project_back(og, w, block=256):
    heads, tokens, _ = og.shape
    rows, columns = w.shape
    return pl.pallas_call(
        back_body,
        grid=(rows // block,),
        in_specs=[pl.BlockSpec((heads, tokens, HD), lambda i: (0, 0, 0)), pl.BlockSpec((block, columns), lambda i: (i, 0))],
        out_specs=pl.BlockSpec((tokens, block), lambda i: (0, i)),
        out_shape=jax.ShapeDtypeStruct((tokens, rows), jnp.bfloat16),
        scratch_shapes=[pltpu.VMEM((tokens, columns), jnp.bfloat16)],
        compiler_params=pltpu.CompilerParams(dimension_semantics=("arbitrary",)),
        name="project_back",
    )(og, w)


def out_body(att, w, out):
    done = dot_nn(att[...], w[...]).astype(out.dtype)
    for h in range(out.shape[0]):
        out[h] = done[:, h * HD:(h + 1) * HD]


def project_out(att, w, block=256):
    tokens, rows = att.shape
    columns = w.shape[1]
    return pl.pallas_call(
        out_body,
        grid=(columns // block,),
        in_specs=[pl.BlockSpec((tokens, rows), lambda i: (0, 0)), pl.BlockSpec((rows, block), lambda i: (0, i))],
        out_specs=pl.BlockSpec((block // HD, tokens, HD), lambda i: (i, 0, 0)),
        out_shape=jax.ShapeDtypeStruct((columns // HD, tokens, HD), jnp.bfloat16),
        compiler_params=pltpu.CompilerParams(dimension_semantics=("arbitrary",)),
        name="project_out",
    )(att, w)

X = "x"
HEAD = ("y", "core")
DP = ("z", "x")


def swap(pieces, axis):
    return lax.all_to_all(pieces, axis, 0, 0, tiled=True)


def everywhere(x, axis):
    return swap(jnp.broadcast_to(x[None], (lax.axis_size(axis), *x.shape)), axis)


def shifted(block, distance):
    size = lax.axis_size(DP)
    return lax.ppermute(block, DP, [(i, i + distance) for i in range(size) if 0 <= i + distance < size])


def on_device(queries, keys, values, output_grad, out_weight, lengths):
    rows = queries.shape[0]
    parts = lax.axis_size(X)
    heads = lax.axis_size(HEAD)
    place = lax.axis_index(DP).astype(jnp.int32).reshape(1)
    own_w = out_weight.reshape(out_weight.shape[0], heads, parts, HD).transpose(2, 0, 1, 3)
    own_w = swap(own_w.reshape(parts, out_weight.shape[0], heads * HD), X)
    weight = lax.all_gather(own_w.reshape(-1, heads * HD), "z", axis=0, tiled=True)
    pair = jnp.concatenate([keys, values], axis=1)
    earlier = [shifted(pair, offset) for offset in (2, 1)]
    grads = swap(output_grad.reshape(rows, parts, HD).transpose(1, 0, 2), X).reshape(parts * rows, HD)
    grads = everywhere(grads, HEAD)
    ks = [e[:, :HD] for e in earlier] + [keys]
    vs = [e[:, HD:] for e in earlier] + [values]
    attended, shares = forward(lengths, place, queries, ks, vs)
    attended_all = everywhere(attended, X).reshape(parts * rows, -1)
    d_parts = project_back(grads, weight).reshape(parts, rows, -1)
    d_parts = swap(d_parts, X)
    projected = swap(project_out(attended_all, weight), HEAD)
    projected = projected.astype(jnp.float32).sum(axis=0).astype(jnp.bfloat16)
    layer_out = swap(projected.reshape(parts, rows, HD), X).transpose(1, 0, 2).reshape(rows, parts * HD)
    query_grad, *returned = backward(queries, ks, vs, d_parts, attended, shares)
    k2, k1, k0, v2, v1, v0 = returned
    two = shifted(jnp.concatenate([k2, v2], axis=1), -2).astype(jnp.float32)
    one = shifted(jnp.concatenate([k1, v1], axis=1), -1).astype(jnp.float32)
    key_grad = k0 + one[:, :HD] + two[:, :HD]
    value_grad = v0 + one[:, HD:] + two[:, HD:]
    return layer_out, query_grad, key_grad.astype(jnp.bfloat16), value_grad.astype(jnp.bfloat16)


def solution(mesh):
    finer = Mesh(mesh.devices.reshape(16, 4, 4, 2), ("z", "x", "y", "core"))
    token = P(DP, HEAD)
    return jax.shard_map(
        on_device,
        mesh=finer,
        in_specs=(token, token, token, token, P(("y", "core", "z", "x"), None), P()),
        out_specs=(token,) * 4,
        check_vma=False,
    )
```

time: 231 us -> 182 us (0.79)
  the two profiles are of different devices: /device:TPU:54 before, /device:TPU:1 now
where the time goes in v2:
time: 182 us; the launch traced here: 181 us
  waiting for transfers between devices  64.6 us (35%)
  starting transfers between devices  40.5 us (22%)
  Pallas kernels  28.5 us (16%)
  blocking collectives  17.5 us (10%)
  between operations  14.2 us (8%)
  local copies, waits for them, and re-layouts  10.8 us (6%)
  other arithmetic  5.2 us (3%)
    all_to_all x5, waiting for transfers between devices, swap(): return lax.all_to_all(pieces, axis, 0, 0, tiled=True)  42.7 us
    all_to_all x5, starting transfers between devices, swap(): return lax.all_to_all(pieces, axis, 0, 0, tiled=True)  32 us
    all_to_all x2, blocking collectives, swap(): return lax.all_to_all(pieces, axis, 0, 0, tiled=True)  17.5 us
    all_gather x1, waiting for transfers between devices, on_device(): lax.all_gather(own_w.reshape(-1, heads * HD), 'z', axis=0, tiled=True)  12.5 us
    ppermute x4, waiting for transfers between devices, shifted(): lax.ppermute(block, DP, [(i, i + distance) for i in range(size) if 0 <= i...  9.41 us
    ppermute x4, starting transfers between devices, shifted(): lax.ppermute(block, DP, [(i, i + distance) for i in range(size) if 0 <= i...  8.47 us
    pallas_call x1, Pallas kernels, backward(): pl.pallas_call(functools.partial(backward_body, 1.0 / math.sqrt(HD), grou...  7.97 us
    pallas_call x1, Pallas kernels, forward(): pl.pallas_call(functools.partial(forward_body, 1.0 / math.sqrt(HD), group...  7.79 us
  transfers between devices with their start and end apart: 10, of which 9 were waited for; matrix products, arithmetic and copies ran while one was open for 5% of the time, Pallas kernels for 16%

profile of v2, /device:TPU:1, one launch (start us, length us, event | category | flops | bytes accessed | tf_op | source)
XLA Modules:
  0.0 181.3 jit_solution(6228916542576304330)
XLA Ops:
  8.3 9.6 %all_to_all.35 = bf16[4,16,1024]{2,1,0:T(8,128)(2,1)} all-to-all(bf16[4,16,1024]{2,1,0:T(8,128)(2,1)S(1)} %reshape.40), channel_id=1, replica_groups=mesh['z'=16,'x'=4,'y'=4,'core'=2] {'x'}, dimensions={0} | all-to-all | bytes 262144 | tf_op jit(solution)/shard_map/all_to_all | solution.py:170
  19.1 7.9 %all_to_all.36 = bf16[4,256,128]{2,1,0:T(8,128)(2,1)S(1)} all-to-all(bf16[4,256,128]{2,1,0:T(8,128)(2,1)S(1)} %copy.24), channel_id=1, replica_groups=mesh['z'=16,'x'=4,'y'=4,'core'=2] {'x'}, dimensions={0} | all-to-all | bytes 524288 | tf_op jit(solution)/shard_map/all_to_all | solution.py:170
  28.7 11.1 %all-to-all-start.5 = ((bf16[8,1024,128]{2,1,0:T(8,128)(2,1)}), bf16[8,1024,128]{2,1,0:T(8,128)(2,1)S(1)}, u32[]{:S(2)}, u32[]{:S(2)}) async-start(bf16[8,1024,128]{2,1,0:T(8,128)(2,1)} %broadcast_in_dim.15), calls=%async_computation.5 | async-start | bytes 4194304 | tf_op jit(solution)/shard_map/all_to_all | solution.py:170
  39.8 2.2 %collective-permute-start.1 = (bf16[256,256]{1,0:T(8,128)(2,1)S(1)}, bf16[256,256]{1,0:T(8,128)(2,1)S(1)}, u32[]{:S(2)}, u32[]{:S(2)}) collective-permute-start(bf16[256,256]{1,0:T(8,128)(2,1)S(1)} %constant_dynamic-update-slice_fusion), channel_id=1, source_target_pairs={{0,8},{8,16},{16,24},{24,32},{32,40},{40,48},{48,56},{56,64},{64,7... | collective-permute-start | bytes 393224 | tf_op jit(solution)/shard_map/ppermute | solution.py:179
  42.1 3.7 %collective-permute-start = (bf16[256,256]{1,0:T(8,128)(2,1)S(1)}, bf16[256,256]{1,0:T(8,128)(2,1)S(1)}, u32[]{:S(2)}, u32[]{:S(2)}) collective-permute-start(bf16[256,256]{1,0:T(8,128)(2,1)S(1)} %constant_dynamic-update-slice_fusion), channel_id=1, source_target_pairs={{0,16},{8,24},{16,32},{24,40},{32,48},{40,56},{48,64},{56,72},{64,... | collective-permute-start | bytes 393224 | tf_op jit(solution)/shard_map/ppermute | solution.py:179
  46.4 1.8 collective-permute-done
  48.8 7.8 %attend_forward.1 = (bf16[256,1024]{1,0:T(8,128)(2,1)}, bf16[8,768,256]{2,1,0:T(8,128)(2,1)}) custom-call(s32[64]{0:T(128)} %lengths.1, s32[1]{0:T(128)} %bitcast.place, bf16[256,1024]{1,0:T(8,128)(2,1)} %refs_0_.1, bf16[256,128]{1,0:T(8,128)(2,1)} %get-tuple-element.39.k2.refs_1_, bf16[256,128]{1,0:T(8,128)(2,1)} %get-tuple-element.37.k1.refs_2_, ...), custom_call_target="tpu_custom_call" | custom-call | tf_op jit(solution)/shard_map/attend_forward/pallas_call | solution.py:56
  56.6 9.4 %all-to-all-done.5.og = bf16[8,1024,128]{2,1,0:T(8,128)(2,1)S(1)} async-done(((bf16[8,1024,128]{2,1,0:T(8,128)(2,1)}), bf16[8,1024,128]{2,1,0:T(8,128)(2,1)S(1)}, u32[]{:S(2)}, u32[]{:S(2)}) %all-to-all-start.5) | async-done | bytes 2097184 | tf_op jit(solution)/shard_map/all_to_all | solution.py:170
  66.0 3.1 %broadcast_in_dim.6 = bf16[4,256,1024]{2,1,0:T(8,128)(2,1)} broadcast(bf16[256,1024]{1,0:T(8,128)(2,1)} %get-tuple-element.13.refs_8_), dimensions={1,2} | broadcast | bytes 2621440 | tf_op jit(solution)/shard_map/broadcast_in_dim | solution.py:174
  69.1 4.4 %all-to-all-start = ((bf16[4,256,1024]{2,1,0:T(8,128)(2,1)}), bf16[4,256,1024]{2,1,0:T(8,128)(2,1)}, u32[]{:S(2)}, u32[]{:S(2)}) async-start(bf16[4,256,1024]{2,1,0:T(8,128)(2,1)} %broadcast_in_dim.6), calls=%async_computation | async-start | bytes 4194304 | tf_op jit(solution)/shard_map/all_to_all | solution.py:170
  73.5 12.5 %all-gather.2.cloned.1.call-done.w = bf16[1024,1024]{1,0:T(8,128)(2,1)} async-done(((bf16[64,1024]{1,0:T(8,128)(2,1)}), bf16[1024,1024]{1,0:T(8,128)(2,1)}) %all-gather.2.cloned.1.call-update) | async-done | bytes 2097168 | tf_op jit(solution)/shard_map/all_gather | solution.py:189
  86.0 6.8 %project_back.1 = bf16[1024,1024]{1,0:T(8,128)(2,1)} custom-call(bf16[8,1024,128]{2,1,0:T(8,128)(2,1)} %copy-done, bf16[1024,1024]{1,0:T(8,128)(2,1)} %all-gather.2.cloned.1.call-done.w), custom_call_target="tpu_custom_call" | custom-call | tf_op jit(solution)/shard_map/project_back/pallas_call | solution.py:133
  92.8 6.3 %all-to-all-done = bf16[4,256,1024]{2,1,0:T(8,128)(2,1)} async-done(((bf16[4,256,1024]{2,1,0:T(8,128)(2,1)}), bf16[4,256,1024]{2,1,0:T(8,128)(2,1)}, u32[]{:S(2)}, u32[]{:S(2)}) %all-to-all-start) | async-done | bytes 2097184 | tf_op jit(solution)/shard_map/all_to_all | solution.py:170
  99.0 3.6 %all-to-all-start.6 = ((bf16[4,256,1024]{2,1,0:T(8,128)(2,1)}), bf16[4,256,1024]{2,1,0:T(8,128)(2,1)S(1)}, u32[]{:S(2)}, u32[]{:S(2)}) async-start(bf16[4,256,1024]{2,1,0:T(8,128)(2,1)} %bitcast.14), calls=%async_computation.6 | async-start | bytes 4194304 | tf_op jit(solution)/shard_map/all_to_all | solution.py:170
  102.7 6.0 %project_out.1 = bf16[8,1024,128]{2,1,0:T(8,128)(2,1)} custom-call(bf16[1024,1024]{1,0:T(8,128)(2,1)} %bitcast.1.att, bf16[1024,1024]{1,0:T(8,128)(2,1)} %all-gather.2.cloned.1.call-done.w), custom_call_target="tpu_custom_call" | custom-call | tf_op jit(solution)/shard_map/project_out/pallas_call | solution.py:154
  108.7 16.0 %all-to-all-done.6.refs_7_ = bf16[4,256,1024]{2,1,0:T(8,128)(2,1)S(1)} async-done(((bf16[4,256,1024]{2,1,0:T(8,128)(2,1)}), bf16[4,256,1024]{2,1,0:T(8,128)(2,1)S(1)}, u32[]{:S(2)}, u32[]{:S(2)}) %all-to-all-start.6) | async-done | bytes 2097184 | tf_op jit(solution)/shard_map/all_to_all | solution.py:170
  126.1 9.5 %all-to-all-start.2 = ((bf16[8,1024,128]{2,1,0:T(8,128)(2,1)}), bf16[8,1024,128]{2,1,0:T(8,128)(2,1)}, u32[]{:S(2)}, u32[]{:S(2)}) async-start(bf16[8,1024,128]{2,1,0:T(8,128)(2,1)} %project_out.1), calls=%async_computation.2 | async-start | bytes 4194304 | tf_op jit(solution)/shard_map/all_to_all | solution.py:170
  135.6 8.0 %attend_backward.1 = (bf16[256,1024]{1,0:T(8,128)(2,1)}, bf16[256,128]{1,0:T(8,128)(2,1)}, bf16[256,128]{1,0:T(8,128)(2,1)}, f32[256,128]{1,0:T(8,128)}, bf16[25...) custom-call(bf16[256,1024]{1,0:T(8,128)(2,1)} %refs_0_.1, ...), custom_call_target="tpu_custom_call" | custom-call | tf_op jit(solution)/shard_map/attend_backward/pallas_call | solution.py:110
  148.0 4.8 %collective-permute-done.3 = bf16[256,256]{1,0:T(8,128)(2,1)S(1)} collective-permute-done((bf16[256,256]{1,0:T(8,128)(2,1)S(1)}, bf16[256,256]{1,0:T(8,128)(2,1)S(1)}, u32[]{:S(2)}, u32[]{:S(2)}) %collective-permute-start.3) | collective-permute-done | bytes 131104 | tf_op jit(solution)/shard_map/ppermute | solution.py:179
  152.8 2.8 %collective-permute-done.2 = bf16[256,256]{1,0:T(8,128)(2,1)S(1)} collective-permute-done((bf16[256,256]{1,0:T(8,128)(2,1)S(1)}, bf16[256,256]{1,0:T(8,128)(2,1)S(1)}, u32[]{:S(2)}, u32[]{:S(2)}) %collective-permute-start.2) | collective-permute-done | bytes 131104 | tf_op jit(solution)/shard_map/ppermute | solution.py:179
  155.7 6.2 %all-to-all-done.2 = bf16[8,1024,128]{2,1,0:T(8,128)(2,1)} async-done(((bf16[8,1024,128]{2,1,0:T(8,128)(2,1)}), bf16[8,1024,128]{2,1,0:T(8,128)(2,1)}, u32[]{:S(2)}, u32[]{:S(2)}) %all-to-all-start.2) | async-done | bytes 2097184 | tf_op jit(solution)/shard_map/all_to_all | solution.py:170
  161.9 2.6 %reduce_sum.12 = bf16[1024,128]{1,0:T(8,128)(2,1)} reduce(bf16[8,1024,128]{2,1,0:T(8,128)(2,1)} %all-to-all-done.2, bf16[]{:T(256)} %constant.15.clone.1), dimensions={0}, to_apply=%region_0.0 | reduce | flops 917504 | bytes 2359298 | tf_op jit(solution)/shard_map/reduce_sum | solution.py:201
  164.6 3.4 %all-to-all-start.3 = ((bf16[4,256,128]{2,1,0:T(8,128)(2,1)}), bf16[4,256,128]{2,1,0:T(8,128)(2,1)S(1)}, u32[]{:S(2)}, u32[]{:S(2)}) async-start(bf16[4,256,128]{2,1,0:T(8,128)(2,1)} %bitcast.4), calls=%async_computation.3 | async-start | bytes 524288 | tf_op jit(solution)/shard_map/all_to_all | solution.py:170
  168.7 4.8 %all-to-all-done.3 = bf16[4,256,128]{2,1,0:T(8,128)(2,1)S(1)} async-done(((bf16[4,256,128]{2,1,0:T(8,128)(2,1)}), bf16[4,256,128]{2,1,0:T(8,128)(2,1)S(1)}, u32[]{:S(2)}, u32[]{:S(2)}) %all-to-all-start.3) | async-done | bytes 262176 | tf_op jit(solution)/shard_map/all_to_all | solution.py:170
  (34 shorter events, 12.9 us)
Async XLA Ops:
  7.2 78.8 %all-gather.2.cloned.1.call-start = ((), (), s32[]{:S(2)}) async-start(), calls=%async_computation.7 | async-start | bytes 2228224 | tf_op jit(solution)/shard_map/all_gather | solution.py:189
  28.7 11.1 %copy-start.2 = (bf16[256,128]{1,0:T(8,128)(2,1)S(1)}, bf16[256,128]{1,0:T(8,128)(2,1)}, u32[]{:S(2)}) copy-start(bf16[256,128]{1,0:T(8,128)(2,1)} %refs_3_.1) | copy-start | bytes 196612
  28.7 11.1 %copy-start.3 = (bf16[256,128]{1,0:T(8,128)(2,1)S(1)}, bf16[256,128]{1,0:T(8,128)(2,1)}, u32[]{:S(2)}) copy-start(bf16[256,128]{1,0:T(8,128)(2,1)} %refs_6_.1) | copy-start | bytes 196612
  28.7 37.3 %all-to-all-start.5 = ((bf16[8,1024,128]{2,1,0:T(8,128)(2,1)}), bf16[8,1024,128]{2,1,0:T(8,128)(2,1)S(1)}, u32[]{:S(2)}, u32[]{:S(2)}) async-start(bf16[8,1024,128]{2,1,0:T(8,128)(2,1)} %broadcast_in_dim.15), calls=%async_computation.5 | async-start | bytes 4194304 | tf_op jit(solution)/shard_map/all_to_all | solution.py:170
  39.8 5.9 %collective-permute-start.1 = (bf16[256,256]{1,0:T(8,128)(2,1)S(1)}, bf16[256,256]{1,0:T(8,128)(2,1)S(1)}, u32[]{:S(2)}, u32[]{:S(2)}) collective-permute-start(bf16[256,256]{1,0:T(8,128)(2,1)S(1)} %constant_dynamic-update-slice_fusion), channel_id=1, source_target_pairs={{0,8},{8,16},{16,24},{24,32},{32,40},{40,48},{48,56},{56,64},{64,7... | collective-permute-start | bytes 393224 | tf_op jit(solution)/shard_map/ppermute | solution.py:179
  42.1 6.1 %collective-permute-start = (bf16[256,256]{1,0:T(8,128)(2,1)S(1)}, bf16[256,256]{1,0:T(8,128)(2,1)S(1)}, u32[]{:S(2)}, u32[]{:S(2)}) collective-permute-start(bf16[256,256]{1,0:T(8,128)(2,1)S(1)} %constant_dynamic-update-slice_fusion), channel_id=1, source_target_pairs={{0,16},{8,24},{16,32},{24,40},{32,48},{40,56},{48,64},{56,72},{64,... | collective-permute-start | bytes 393224 | tf_op jit(solution)/shard_map/ppermute | solution.py:179
  66.0 3.1 %copy-start = (bf16[8,1024,128]{2,1,0:T(8,128)(2,1)}, bf16[8,1024,128]{2,1,0:T(8,128)(2,1)S(1)}, u32[]{:S(2)}) copy-start(bf16[8,1024,128]{2,1,0:T(8,128)(2,1)S(1)} %all-to-all-done.5.og) | copy-start | bytes 6291460
  69.1 30.0 %all-to-all-start = ((bf16[4,256,1024]{2,1,0:T(8,128)(2,1)}), bf16[4,256,1024]{2,1,0:T(8,128)(2,1)}, u32[]{:S(2)}, u32[]{:S(2)}) async-start(bf16[4,256,1024]{2,1,0:T(8,128)(2,1)} %broadcast_in_dim.6), calls=%async_computation | async-start | bytes 4194304 | tf_op jit(solution)/shard_map/all_to_all | solution.py:170
  99.0 25.6 %all-to-all-start.6 = ((bf16[4,256,1024]{2,1,0:T(8,128)(2,1)}), bf16[4,256,1024]{2,1,0:T(8,128)(2,1)S(1)}, u32[]{:S(2)}, u32[]{:S(2)}) async-start(bf16[4,256,1024]{2,1,0:T(8,128)(2,1)} %bitcast.14), calls=%async_computation.6 | async-start | bytes 4194304 | tf_op jit(solution)/shard_map/all_to_all | solution.py:170
  124.7 1.4 copy-start.1
  126.1 35.8 %all-to-all-start.2 = ((bf16[8,1024,128]{2,1,0:T(8,128)(2,1)}), bf16[8,1024,128]{2,1,0:T(8,128)(2,1)}, u32[]{:S(2)}, u32[]{:S(2)}) async-start(bf16[8,1024,128]{2,1,0:T(8,128)(2,1)} %project_out.1), calls=%async_computation.2 | async-start | bytes 4194304 | tf_op jit(solution)/shard_map/all_to_all | solution.py:170
  143.5 24.4 %copy-start.4 = (f32[256,128]{1,0:T(8,128)S(1)}, f32[256,128]{1,0:T(8,128)}, u32[]{:S(2)}) copy-start(f32[256,128]{1,0:T(8,128)} %get-tuple-element.16) | copy-start | bytes 393220
  143.5 24.4 %copy-start.5 = (f32[256,128]{1,0:T(8,128)S(1)}, f32[256,128]{1,0:T(8,128)}, u32[]{:S(2)}) copy-start(f32[256,128]{1,0:T(8,128)} %get-tuple-element.21) | copy-start | bytes 393220
  144.5 8.3 %collective-permute-start.3 = (bf16[256,256]{1,0:T(8,128)(2,1)S(1)}, bf16[256,256]{1,0:T(8,128)(2,1)S(1)}, u32[]{:S(2)}, u32[]{:S(2)}) collective-permute-start(bf16[256,256]{1,0:T(8,128)(2,1)S(1)} %pad_maximum_fusion.1), channel_id=1, source_target_pairs={{16,0},{24,8},{32,16},{40,24},{48,32},{56,40},{64,48},{72,56},{80,... | collective-permute-start | bytes 393224 | tf_op jit(solution)/shard_map/ppermute | solution.py:179
  146.7 9.0 %collective-permute-start.2 = (bf16[256,256]{1,0:T(8,128)(2,1)S(1)}, bf16[256,256]{1,0:T(8,128)(2,1)S(1)}, u32[]{:S(2)}, u32[]{:S(2)}) collective-permute-start(bf16[256,256]{1,0:T(8,128)(2,1)S(1)} %pad_maximum_fusion), channel_id=1, source_target_pairs={{8,0},{16,8},{24,16},{32,24},{40,32},{48,40},{56,48},{64,56},{72,6... | collective-permute-start | bytes 393224 | tf_op jit(solution)/shard_map/ppermute | solution.py:179
  164.6 8.9 %all-to-all-start.3 = ((bf16[4,256,128]{2,1,0:T(8,128)(2,1)}), bf16[4,256,128]{2,1,0:T(8,128)(2,1)S(1)}, u32[]{:S(2)}, u32[]{:S(2)}) async-start(bf16[4,256,128]{2,1,0:T(8,128)(2,1)} %bitcast.4), calls=%async_computation.3 | async-start | bytes 524288 | tf_op jit(solution)/shard_map/all_to_all | solution.py:170
Sparse Core Ops, SparseCore 0:
  18.0 67.9 all-gather.1
